TPU v7x, 32 devices: a whole 2x2x4 slice. The times are simulated.
32 devices in a mesh: ctx: 8 (over z, y), tile: 4 (over x, core).
Axes of the slice: x: 2, y: 2, z: 4, core: 2. Of those that a mesh axis runs over, the one named last changes fastest.
Arguments:
- masks: bfloat16 [16, 512, 512], P('ctx', 'tile'), may hold values from 0 to 1
- blur_rows: bfloat16 [512, 512], replicated, may hold values from -0.25 to 0.25
- blur_cols: bfloat16 [512, 512], replicated, may hold values from -0.25 to 0.25
- pupils: float32 [6, 64, 128], replicated, may hold values from -5 to 5
- targets: bfloat16 [16, 512, 512], P('ctx', 'tile'), may hold values from 0 to 1
- context_masters: int32 [16, 12], P('ctx'), may hold values from 0 to 15, as said below
- offsets: int32 [16, 12, 2], P('ctx'), may hold values from 0 to 511
Outputs:
- resist: bfloat16 [16, 512, 512], P('ctx', 'tile')
- mask_grad: float32 [16, 512, 512], P('ctx', 'tile')
Inputs may be any that keep to these rules, and one draw needn't show every extreme that they name: `context_masters`: master m lies on ctx index m // 2. Among the masters named by the 2 contexts of one ctx index there is at most one lying on any one ctx index; a master may be named several times.
All inputs are finite; a program needn't handle non-finite values.
Results may differ from a plain program's by a relative error of at most 0.019.
Values may be sent and summed in bfloat16 or wider, within the bound.
No kernel may reach another device: no remote copies, remote signals or barrier semaphores. Data moves between devices by JAX's collectives and lax.ppermute only.
A program may use at most 64 MiB of HBM per device.

v0:
```python
import math
import jax
import jax.numpy as jnp
from jax import lax
from jax.sharding import PartitionSpec as P

STEEPNESS = 4.0
THRESHOLD = 1.0


def build_tables(extent, mode_count):
    frequency = (jnp.arange(mode_count, dtype=jnp.int32) - mode_count // 2) % extent
    positions = jnp.arange(extent, dtype=jnp.int32)
    windings = frequency[:, None] * positions[None, :] % extent
    angles = windings.astype(jnp.float32) * (2.0 * math.pi / extent)
    scale_factor = 1.0 / math.sqrt(extent)
    cosine_table = jnp.cos(angles) * scale_factor
    sine_table = jnp.sin(angles) * scale_factor
    row_real = cosine_table.astype(jnp.bfloat16)
    row_imag = (-sine_table).astype(jnp.bfloat16)
    col_fwd = jnp.concatenate([cosine_table.T, -sine_table.T], axis=1).astype(jnp.bfloat16)
    inverse_big = jnp.concatenate(
        [
            jnp.concatenate([cosine_table, sine_table], axis=1),
            jnp.concatenate([-sine_table, cosine_table], axis=1),
        ],
        axis=0,
    ).astype(jnp.bfloat16)
    back_real = cosine_table.T.astype(jnp.bfloat16)
    back_imag = sine_table.T.astype(jnp.bfloat16)
    adjoint_big = jnp.concatenate(
        [
            jnp.concatenate([cosine_table.T, -sine_table.T], axis=1),
            jnp.concatenate([sine_table.T, cosine_table.T], axis=1),
        ],
        axis=0,
    ).astype(jnp.bfloat16)
    return (row_real, row_imag, col_fwd, inverse_big, back_real, back_imag, adjoint_big)


def complex_left(left_real, left_imag, values):
    width = values.shape[-1] // 2
    real_lead = jnp.einsum("ux,...xv->...uv", left_real, values, preferred_element_type=jnp.float32)
    imag_lead = jnp.einsum("ux,...xv->...uv", left_imag, values, preferred_element_type=jnp.float32)
    return jnp.concatenate(
        [
            real_lead[..., :width] - imag_lead[..., width:],
            real_lead[..., width:] + imag_lead[..., :width],
        ],
        axis=-1,
    )


def complex_times(factor, values, conjugate):
    width = values.shape[-1] // 2
    factor_real = factor[..., :width]
    factor_imag = factor[..., width:]
    if conjugate:
        factor_imag = -factor_imag
    values_real = values[..., :width]
    values_imag = values[..., width:]
    return jnp.concatenate(
        [
            factor_real * values_real - factor_imag * values_imag,
            factor_real * values_imag + factor_imag * values_real,
        ],
        axis=-1,
    )


def phase_table(shifts, row_begin, band_rows, mode_count, extent):
    freq_u = (jnp.arange(band_rows, dtype=jnp.int32) + row_begin - mode_count // 2) % extent
    freq_v = (jnp.arange(mode_count, dtype=jnp.int32) - mode_count // 2) % extent
    windings = (
        freq_u[None, :, None] * shifts[:, 0][:, None, None]
        + freq_v[None, None, :] * shifts[:, 1][:, None, None]
    ) % extent
    angles = windings.astype(jnp.float32) * (2.0 * math.pi / extent)
    return jnp.concatenate([jnp.cos(angles), -jnp.sin(angles)], axis=-1)


def image_adjoint(
    spectrum, target, pupils, back_real, back_imag, row_real, row_imag, inverse_big, adjoint_big
):
    amplitude = complex_times(pupils, spectrum[None], False).astype(jnp.bfloat16)
    spread = jnp.einsum(
        "kuv,vy->kuy", amplitude, inverse_big, preferred_element_type=jnp.float32
    ).astype(jnp.bfloat16)
    field = complex_left(back_real, back_imag, spread)
    width = field.shape[-1] // 2
    field_real = field[..., :width]
    field_imag = field[..., width:]
    intensity = jnp.sum(field_real * field_real + field_imag * field_imag, axis=0)
    resist = jax.nn.sigmoid(STEEPNESS * (intensity - THRESHOLD))
    slope_term = (resist - target.astype(jnp.float32)) * STEEPNESS * resist * (1.0 - resist)
    pull_back = jnp.concatenate(
        [2.0 * slope_term * field_real, 2.0 * slope_term * field_imag], axis=-1
    ).astype(jnp.bfloat16)
    folded = jnp.einsum(
        "kxy,yv->kxv", pull_back, adjoint_big, preferred_element_type=jnp.float32
    ).astype(jnp.bfloat16)
    grad_amp = complex_left(row_real, row_imag, folded)
    grad_spec = jnp.sum(complex_times(pupils, grad_amp, True), axis=0)
    return (resist.astype(jnp.bfloat16), grad_spec)


def local(masks, blur_rows, blur_cols, pupils, targets, context_masters, offsets):
    ctx_count = lax.axis_size("ctx")
    owned, row_count, extent = masks.shape
    mode_count = pupils.shape[1]
    context_count = context_masters.shape[0]
    source_count = context_masters.shape[1]
    tile_pos = lax.axis_index("tile")
    row_start = tile_pos * row_count
    row_real, row_imag, col_fwd, inverse_big, back_real, back_imag, adjoint_big = build_tables(
        extent, mode_count
    )
    own_row_real = lax.dynamic_slice_in_dim(row_real, row_start, row_count, 1)
    own_row_imag = lax.dynamic_slice_in_dim(row_imag, row_start, row_count, 1)
    own_back_real = lax.dynamic_slice_in_dim(back_real, row_start, row_count, 0)
    own_back_imag = lax.dynamic_slice_in_dim(back_imag, row_start, row_count, 0)
    own_blur = lax.dynamic_slice_in_dim(blur_rows, row_start, row_count, 0)
    own_blur_cols = lax.dynamic_slice_in_dim(blur_rows, row_start, row_count, 1)
    owners = (context_masters // owned).reshape(-1)
    local_index = (context_masters % owned).reshape(-1)
    slot_index = jnp.arange(ctx_count, dtype=jnp.int32)
    owner_match = owners[:, None] == slot_index[None, :]
    wanted = jnp.max(jnp.where(owner_match, local_index[:, None] + 1, 0), axis=0)
    asked_for = lax.all_to_all(wanted[:, None], "ctx", split_axis=0, concat_axis=0, tiled=True)[
        :, 0
    ]
    chosen = asked_for[:, None] == jnp.arange(owned, dtype=jnp.int32)[None, :] + 1
    half_blur = jnp.einsum(
        "mxy,zy->mxz", masks, blur_cols, preferred_element_type=jnp.float32
    ).astype(jnp.bfloat16)
    weights = own_blur
    blurred = jnp.einsum(
        "xj,mjz->mxz",
        weights,
        lax.all_gather(half_blur, "tile", axis=1, tiled=True),
        preferred_element_type=jnp.float32,
    ).astype(jnp.bfloat16)
    column = jnp.einsum("mxy,yv->mxv", blurred, col_fwd, preferred_element_type=jnp.float32).astype(
        jnp.bfloat16
    )
    partial_value = complex_left(own_row_real, own_row_imag, column)
    spectra = lax.psum(partial_value.astype(jnp.bfloat16), "tile")
    outgoing = jnp.einsum(
        "dm,muv->duv", chosen.astype(jnp.bfloat16), spectra, preferred_element_type=jnp.float32
    ).astype(jnp.bfloat16)
    incoming = lax.all_to_all(outgoing, "ctx", split_axis=0, concat_axis=0, tiled=True)
    flat_shift = offsets.reshape(-1, 2)
    picked = jnp.take(incoming, owners, axis=0).astype(jnp.float32)
    turned = complex_times(
        phase_table(flat_shift, 0, mode_count, mode_count, extent), picked, False
    )
    context_spec = jnp.sum(
        turned.reshape(context_count, source_count, mode_count, 2 * mode_count), axis=1
    )

    def one_context(inputs):
        spectrum, target = inputs
        return image_adjoint(
            spectrum,
            target,
            pupils,
            own_back_real,
            own_back_imag,
            own_row_real,
            own_row_imag,
            inverse_big,
            adjoint_big,
        )

    resist, grad_part = lax.map(one_context, (context_spec, targets))
    grad_ctx = lax.psum(grad_part.astype(jnp.bfloat16), "tile").astype(jnp.float32)
    band_start = 0
    repeated = jnp.repeat(grad_ctx, source_count, axis=0)
    back_turn = complex_times(
        phase_table(flat_shift, band_start, mode_count, mode_count, extent), repeated, True
    )
    returned = jnp.einsum(
        "rd,ruv->duv", owner_match.astype(jnp.float32), back_turn, precision=lax.Precision.HIGHEST
    )
    arrived = lax.all_to_all(
        returned.astype(jnp.bfloat16), "ctx", split_axis=0, concat_axis=0, tiled=True
    ).astype(returned.dtype)
    master_grad = jnp.einsum(
        "dm,duv->muv", chosen.astype(jnp.float32), arrived, precision=lax.Precision.HIGHEST
    ).astype(jnp.bfloat16)
    lifted = jnp.einsum(
        "muv,vy->muy", master_grad, inverse_big, preferred_element_type=jnp.float32
    ).astype(jnp.bfloat16)
    surface = (
        jnp.einsum(
            "xu,muy->mxy", own_back_real, lifted[..., :extent], preferred_element_type=jnp.float32
        )
        - jnp.einsum(
            "xu,muy->mxy", own_back_imag, lifted[..., extent:], preferred_element_type=jnp.float32
        )
    ).astype(jnp.bfloat16)
    settled = jnp.einsum(
        "mxy,yz->mxz", surface, blur_cols, preferred_element_type=jnp.float32
    ).astype(jnp.bfloat16)
    weights = own_blur_cols
    mask_grad = jnp.einsum(
        "jx,mjz->mxz",
        weights,
        lax.all_gather(settled, "tile", axis=1, tiled=True),
        preferred_element_type=jnp.float32,
    )
    return (resist, mask_grad)


def solution(mesh):
    placed = (
        P("ctx", "tile", None),
        P(),
        P(),
        P(),
        P("ctx", "tile", None),
        P("ctx", None),
        P("ctx", None, None),
    )
    return jax.shard_map(
        local,
        mesh=mesh,
        in_specs=placed,
        out_specs=(P("ctx", "tile", None), P("ctx", "tile", None)),
        check_vma=False,
    )
```

profile of v0, /device:TPU:0, one launch (start us, length us, event | category | flops | bytes accessed | tf_op | source)
XLA Modules:
  0.0 133.8 jit_solution(16642103256916884030)
XLA Ops:
  7.2 1.0 copy-done
  8.2 2.0 %convolution_convert_fusion.4 = bf16[2,128,512]{2,1,0:T(8,128)(2,1)} fusion(bf16[2,128,512]{2,1,0:T(8,128)(2,1)} %param.9, bf16[512,512]{1,0:T(8,128)(2,1)S(1)} %copy-done), kind=kOutput, calls=%fused_computation.57 | convolution fusion | flops 134348800 | bytes 1048576 | tf_op jit(solution)/shard_map/mxy,zy->mxz/dot_general | solution.py:133
  10.2 0.7 and_select_fusion.1
  11.3 0.7 copy.75
  11.9 7.3 %all-to-all-start = ((s32[8,1,1]{2,1,0:T(1,128)}), s32[8,1,1]{2,1,0:T(1,128)S(1)}, u32[]{:S(2)}, u32[]{:S(2)}) async-start(s32[8,1,1]{2,1,0:T(1,128)} %copy.75), calls=%async_computation | async-start | bytes 8192 | tf_op jit(solution)/shard_map/all_to_all | solution.py:129
  19.3 0.7 copy.73
  20.1 1.1 fusion.45
  22.2 1.1 cosine_multiply_fusion
  23.7 2.0 %all-to-all-done = s32[8,1,1]{2,1,0:T(1,128)S(1)} async-done(((s32[8,1,1]{2,1,0:T(1,128)}), s32[8,1,1]{2,1,0:T(1,128)S(1)}, u32[]{:S(2)}, u32[]{:S(2)}) %all-to-all-start) | async-done | bytes 64 | tf_op jit(solution)/shard_map/all_to_all | solution.py:129
  26.0 3.9 %all-gather.3.cloned.1.call-done = bf16[2,512,512]{2,1,0:T(8,128)(2,1)} async-done(((bf16[2,128,512]{2,1,0:T(8,128)(2,1)}), bf16[2,512,512]{2,1,0:T(8,128)(2,1)}) %all-gather.3.cloned.1.call-update) | async-done | bytes 1048592 | tf_op jit(solution)/shard_map/all_gather | solution.py:140
  29.9 1.9 %fusion.26 = bf16[2,128,128]{2,1,0:T(8,128)(2,1)S(1)} fusion(bf16[2,512,512]{2,1,0:T(8,128)(2,1)} %all-gather.3.cloned.1.call-done, bf16[512,128]{1,0:T(8,128)(2,1)S(1)} %maximum_convert_fusion, bf16[512,512]{1,0:T(8,128)(2,1)S(1)} %copy-done.5, s32[]{:T(128)S(6)} %select_n.140), kind=kOutput, calls=%fused_computation.65 | convolution fusion | flops 167936000 | bytes 1376260 | tf_op jit(solution)/shard_map/mxy,yv->mxv/dot_general | solution.py:143
  32.3 10.4 %psum.14 = bf16[2,64,128]{2,1,0:T(8,128)(2,1)S(1)} all-reduce(bf16[2,64,128]{2,1,0:T(8,128)(2,1)S(1)} %pad_maximum_fusion.1), channel_id=1, replica_groups=mesh['ctx'=8,'tile'=4] {'tile'}, use_global_device_ids=true, to_apply=%region_1.2 | all-reduce | flops 16384 | bytes 65536 | tf_op jit(solution)/shard_map/psum | solution.py:147
  43.0 0.7 copy.79
  43.6 5.7 %all-to-all-start.1 = ((bf16[8,64,128]{2,1,0:T(8,128)(2,1)}), bf16[8,64,128]{2,1,0:T(8,128)(2,1)S(1)}, u32[]{:S(2)}, u32[]{:S(2)}) async-start(bf16[8,64,128]{2,1,0:T(8,128)(2,1)} %copy.79), calls=%async_computation.1 | async-start | bytes 262144 | tf_op jit(solution)/shard_map/all_to_all | solution.py:151
  49.5 7.2 %all-to-all-done.1 = bf16[8,64,128]{2,1,0:T(8,128)(2,1)S(1)} async-done(((bf16[8,64,128]{2,1,0:T(8,128)(2,1)}), bf16[8,64,128]{2,1,0:T(8,128)(2,1)S(1)}, u32[]{:S(2)}, u32[]{:S(2)}) %all-to-all-start.1) | async-done | bytes 131104 | tf_op jit(solution)/shard_map/all_to_all | solution.py:151
  57.6 4.6 %multiply_subtract_fusion.2 = (f32[24,64,64]{2,0,1:T(8,128)S(1)}, f32[24,64,64]{2,0,1:T(8,128)S(1)}) fusion(f32[24,64,128]{2,0,1:T(8,128)S(1)} %fusion.35, s32[24,64]{1,0:T(8,128)S(1)} %get-tuple-element.289, s32[24,64]{0,1:T(8,128)S(1)} %copy.74), kind=kLoop, calls=%fused_computation.79 | loop fusion | flops 2064384 | bytes 1585152 | tf_op jit(solution)/shard_map/sub | solution.py:64
  62.7 0.7 copy-done.4
  63.4 19.3 %while.14 = (s32[]{:T(128)}, bf16[2,128,512]{2,1,0:T(8,128)(2,1)}, bf16[2,64,128]{2,1,0:T(8,128)(2,1)S(1)}, f32[6,64,128]{2,1,0:T(8,128)S(1)}, f32[2,64,128]{2,1...) while((s32[]{:T(128)}, bf16[2,128,512]{2,1,0:T(8,128)(2,1)}, ...), condition=%wide.region_6.7_spmd, body=%wide.region_3.6_spmd.sunk | while | flops 538632192 | bytes 57360672 | solution.py:175
  64.7 0.6 convolution_bitcast_fusion.12
  65.3 1.0 copy-done.1
  66.8 1.2 copy-done.2
  68.5 3.3 %multiply_convert_fusion.4 = (bf16[6,128,512]{1,2,0:T(8,128)(2,1)S(1)}, bf16[6,128,512]{1,2,0:T(8,128)(2,1)S(1)}) fusion(f32[128,512]{0,1:T(8,128)S(1)} %fusion.130, f32[6,128,1024]{1,2,0:T(8,128)} %copy-done.1, f32[6,128,1024]{1,2,0:T(8,128)} %copy-done.2), kind=kLoop, calls=%fused_computation.10.clone.1 | loop fusion | flops 2359296 | bytes 8126464 | tf_op jit(solution)/shard_map/convert
  75.0 1.0 copy-done.1
  76.4 1.2 copy-done.2
  78.2 3.3 %multiply_convert_fusion.4 = (bf16[6,128,512]{1,2,0:T(8,128)(2,1)S(1)}, bf16[6,128,512]{1,2,0:T(8,128)(2,1)S(1)}) fusion(f32[128,512]{0,1:T(8,128)S(1)} %fusion.130, f32[6,128,1024]{1,2,0:T(8,128)} %copy-done.1, f32[6,128,1024]{1,2,0:T(8,128)} %copy-done.2), kind=kLoop, calls=%fused_computation.10.clone.1 | loop fusion | flops 2359296 | bytes 8126464 | tf_op jit(solution)/shard_map/convert
  82.8 10.4 %psum.15 = bf16[2,64,128]{2,1,0:T(8,128)(2,1)S(1)} all-reduce(bf16[2,64,128]{2,1,0:T(8,128)(2,1)S(1)} %get-tuple-element.159), channel_id=1, replica_groups=mesh['ctx'=8,'tile'=4] {'tile'}, use_global_device_ids=true, to_apply=%region_7.8 | all-reduce | flops 16384 | bytes 65536 | tf_op jit(solution)/shard_map/psum | solution.py:176
  93.6 3.7 %multiply_subtract_fusion.1 = (f32[24,64,64]{2,0,1:T(8,128)S(1)}, f32[24,64,64]{2,0,1:T(8,128)S(1)}) fusion(f32[24,64,64]{2,1,0:T(8,128)S(1)} %get-tuple-element.276, f32[24,64,64]{2,1,0:T(8,128)S(1)} %get-tuple-element.275, s32[24,64]{1,0:T(8,128)S(1)} %get-tuple-element.289, s32[24,64]{0,1:T(8,128)S(1)} %copy.74), kind=kLoop, calls=%fused_computation.77 | loop fusion | flops 1966080 | bytes 1585152 | tf_op jit(solution)/shard_map/sub | solution.py:64
  97.8 9.9 %all_to_all.19 = bf16[8,64,128]{2,1,0:T(8,128)(2,1)S(1)} all-to-all(bf16[8,64,128]{2,1,0:T(8,128)(2,1)S(1)} %copy.87), channel_id=1, replica_groups=mesh['ctx'=8,'tile'=4] {'ctx'}, dimensions={0} | all-to-all | bytes 262144 | tf_op jit(solution)/shard_map/all_to_all | solution.py:185
  108.5 1.3 %convolution_convert_fusion.1 = bf16[2,128,512]{2,1,0:T(8,128)(2,1)} fusion(f32[2,512,128]{2,1,0:T(8,128)S(1)} %fusion.52, bf16[512,512]{1,0:T(8,128)(2,1)S(1)} %copy-done, bf16[2,64,1024]{2,1,0:T(8,128)(2,1)S(1)} %convolution_convert_fusion.2, bf16[128,64]{1,0:T(8,128)(2,1)S(1)} %constant_dynamic-slice_fusion.1), kind=kOutput, calls=%fused_computation.54 | convolution fusion | flops 151388160 | bytes 1474560 | tf_op jit(solution)/shard_map/mxy,yz->mxz/dot_general | solution.py:202
  109.8 14.5 %all-gather.5.cloned.1.call-done = bf16[2,512,512]{2,1,0:T(8,128)(2,1)} async-done(((bf16[2,128,512]{2,1,0:T(8,128)(2,1)}), bf16[2,512,512]{2,1,0:T(8,128)(2,1)}) %all-gather.5.cloned.1.call-update) | async-done | bytes 1048592 | tf_op jit(solution)/shard_map/all_gather | solution.py:209
  124.3 1.7 %convolution_bitcast_fusion.4 = f32[2,128,512]{1,2,0:T(8,128)S(1)} fusion(bf16[2,512,512]{2,1,0:T(8,128)(2,1)} %all-gather.5.cloned.1.call-done, bf16[512,512]{1,0:T(8,128)(2,1)S(1)} %copy-done.5, s32[]{:T(128)S(6)} %select_n.140), kind=kOutput, calls=%fused_computation.51 | convolution fusion | flops 134217728 | bytes 1703940 | tf_op jit(solution)/shard_map/jx,mjz->mxz/dot_general | solution.py:206
  126.0 1.0 copy.95
  (98 shorter events, 13.3 us)
Async XLA Ops:
  7.2 1.0 copy-start
  7.2 22.7 %all-gather.3.cloned.1.call-start = ((), (), s32[]{:S(2)}) async-start(), calls=%async_computation.3 | async-start | bytes 1310720 | tf_op jit(solution)/shard_map/all_gather | solution.py:140
  10.2 19.7 %copy-start.5 = (bf16[512,512]{1,0:T(8,128)(2,1)S(1)}, bf16[512,512]{1,0:T(8,128)(2,1)}, u32[]{:S(2)}) copy-start(bf16[512,512]{1,0:T(8,128)(2,1)} %param.10) | copy-start | bytes 1572868
  11.9 13.8 %all-to-all-start = ((s32[8,1,1]{2,1,0:T(1,128)}), s32[8,1,1]{2,1,0:T(1,128)S(1)}, u32[]{:S(2)}, u32[]{:S(2)}) async-start(s32[8,1,1]{2,1,0:T(1,128)} %copy.75), calls=%async_computation | async-start | bytes 8192 | tf_op jit(solution)/shard_map/all_to_all | solution.py:129
  23.6 25.8 %copy-start.3 = (f32[6,64,128]{2,1,0:T(8,128)S(1)}, f32[6,64,128]{2,1,0:T(8,128)}, u32[]{:S(2)}) copy-start(f32[6,64,128]{2,1,0:T(8,128)} %param.12) | copy-start | bytes 589828
  43.6 13.0 %all-to-all-start.1 = ((bf16[8,64,128]{2,1,0:T(8,128)(2,1)}), bf16[8,64,128]{2,1,0:T(8,128)(2,1)S(1)}, u32[]{:S(2)}, u32[]{:S(2)}) async-start(bf16[8,64,128]{2,1,0:T(8,128)(2,1)} %copy.79), calls=%async_computation.1 | async-start | bytes 262144 | tf_op jit(solution)/shard_map/all_to_all | solution.py:151
  49.3 75.0 %all-gather.5.cloned.1.call-start = ((), (), s32[]{:S(2)}) async-start(), calls=%async_computation.4 | async-start | bytes 1310720 | tf_op jit(solution)/shard_map/all_gather | solution.py:209
  62.5 1.0 copy-start.4
  64.7 1.6 %copy-start.1 = (f32[6,128,1024]{1,2,0:T(8,128)}, f32[6,128,1024]{1,2,0:T(8,128)S(1)}, u32[]{:S(2)}) copy-start(f32[6,128,1024]{1,2,0:T(8,128)S(1)} %convolution_bitcast_fusion.11) | copy-start | bytes 9437188 | tf_op jit(solution)/shard_map/while
  66.3 1.7 %copy-start.2 = (f32[6,128,1024]{1,2,0:T(8,128)}, f32[6,128,1024]{1,2,0:T(8,128)S(1)}, u32[]{:S(2)}) copy-start(f32[6,128,1024]{1,2,0:T(8,128)S(1)} %convolution_bitcast_fusion.12) | copy-start | bytes 9437188 | tf_op jit(solution)/shard_map/while
  66.3 1.9 %copy-start.6 = (bf16[2,128,512]{2,1,0:T(8,128)(2,1)S(1)}, bf16[2,128,512]{2,1,0:T(8,128)(2,1)}, u32[]{:S(2)}) copy-start(bf16[2,128,512]{2,1,0:T(8,128)(2,1)} %get-tuple-element.410) | copy-start | bytes 786436 | tf_op jit(solution)/shard_map/while
  68.2 3.6 %copy-start.7 = (bf16[2,128,512]{2,1,0:T(8,128)(2,1)}, bf16[2,128,512]{2,1,0:T(8,128)(2,1)S(1)}, u32[]{:S(2)}) copy-start(bf16[2,128,512]{2,1,0:T(8,128)(2,1)S(1)} %get-tuple-element.426) | copy-start | bytes 786436 | tf_op jit(solution)/shard_map/while
  74.4 1.6 %copy-start.1 = (f32[6,128,1024]{1,2,0:T(8,128)}, f32[6,128,1024]{1,2,0:T(8,128)S(1)}, u32[]{:S(2)}) copy-start(f32[6,128,1024]{1,2,0:T(8,128)S(1)} %convolution_bitcast_fusion.11) | copy-start | bytes 9437188 | tf_op jit(solution)/shard_map/while
  76.0 1.7 %copy-start.2 = (f32[6,128,1024]{1,2,0:T(8,128)}, f32[6,128,1024]{1,2,0:T(8,128)S(1)}, u32[]{:S(2)}) copy-start(f32[6,128,1024]{1,2,0:T(8,128)S(1)} %convolution_bitcast_fusion.12) | copy-start | bytes 9437188 | tf_op jit(solution)/shard_map/while
  76.0 1.9 %copy-start.6 = (bf16[2,128,512]{2,1,0:T(8,128)(2,1)S(1)}, bf16[2,128,512]{2,1,0:T(8,128)(2,1)}, u32[]{:S(2)}) copy-start(bf16[2,128,512]{2,1,0:T(8,128)(2,1)} %get-tuple-element.410) | copy-start | bytes 786436 | tf_op jit(solution)/shard_map/while
  77.9 3.6 %copy-start.7 = (bf16[2,128,512]{2,1,0:T(8,128)(2,1)}, bf16[2,128,512]{2,1,0:T(8,128)(2,1)S(1)}, u32[]{:S(2)}) copy-start(bf16[2,128,512]{2,1,0:T(8,128)(2,1)S(1)} %get-tuple-element.426) | copy-start | bytes 786436 | tf_op jit(solution)/shard_map/while
Sparse Core Ops, SparseCore 0:
  10.3 19.4 all-gather.2
  110.0 14.2 all-gather.4
where the time goes:
time: 134 us
  blocking collectives  30.8 us (23%)
  waiting for transfers between devices  27.6 us (21%)
  other arithmetic  22.2 us (17%)
  between operations  14.3 us (11%)
  matrix products  13.9 us (10%)
  starting transfers between devices  13.1 us (10%)
  local copies, waits for them, and re-layouts  11.7 us (9%)
    all_gather x1, waiting for transfers between devices, local(): lax.all_gather(settled, 'tile', axis=1, tiled=True)  14.5 us
    psum x1, blocking collectives, local(): lax.psum(grad_part.astype(jnp.bfloat16), 'tile').astype(jnp.float32)  10.4 us
    psum x1, blocking collectives, local(): spectra = lax.psum(partial_value.astype(jnp.bfloat16), 'tile')  10.4 us
    all_to_all x1, blocking collectives, local(): lax.all_to_all(returned.astype(jnp.bfloat16), 'ctx', split_axis=0, concat...  9.92 us
    sub x4, other arithmetic, complex_times(): factor_real * values_real - factor_imag * values_imag  8.65 us
    another operation x6, other arithmetic  7.55 us
    all_to_all x1, starting transfers between devices, local(): lax.all_to_all(wanted[:, None], 'ctx', split_axis=0, concat_axis=0, tiled...  7.31 us
    all_to_all x1, waiting for transfers between devices, local(): lax.all_to_all(outgoing, 'ctx', split_axis=0, concat_axis=0, tiled=True)  7.17 us
  transfers between devices with their start and end apart: 4, of which 4 were waited for; matrix products, arithmetic and copies ran while one was open for 5% of the time, Pallas kernels for 0%

commit v1 on v0

--- a/solution.py
+++ b/solution.py
@@ -203,12 +203,39 @@
         "mxy,yz->mxz", surface, blur_cols, preferred_element_type=jnp.float32
     ).astype(jnp.bfloat16)
     weights = own_blur_cols
+    p_next = jax.lax.axis_size("tile")
+    spare, val2, e_now = (p_next, jax.lax.axis_index("tile"), settled.shape[1])
+    slots = tuple(((kk, (kk + 1) % spare) for kk in range(spare)))
+    steps_seen = tuple(((kk, (kk - 1) % spare) for kk in range(spare)))
+    w_next = f_now = settled
+    inter = spare // 2
+    q = 1
     mask_grad = jnp.einsum(
         "jx,mjz->mxz",
-        weights,
-        lax.all_gather(settled, "tile", axis=1, tiled=True),
+        lax.dynamic_slice_in_dim(weights, val2 * e_now, settled.shape[1], axis=0),
+        settled,
         preferred_element_type=jnp.float32,
     )
+    while q < inter + 1:
+        w_next = jax.lax.ppermute(w_next, axis_name="tile", perm=slots)
+        if q < spare - inter:
+            f_now = jax.lax.ppermute(f_now, axis_name="tile", perm=steps_seen)
+            small = jnp.einsum(
+                "jx,mjz->mxz",
+                lax.dynamic_slice_in_dim(
+                    weights, (val2 + q) % spare * e_now, f_now.shape[1], axis=0
+                ),
+                f_now,
+                preferred_element_type=jnp.float32,
+            )
+            mask_grad = mask_grad + small
+        mask_grad = mask_grad + jnp.einsum(
+            "jx,mjz->mxz",
+            lax.dynamic_slice_in_dim(weights, (val2 - q) % spare * e_now, w_next.shape[1], axis=0),
+            w_next,
+            preferred_element_type=jnp.float32,
+        )
+        q = q + 1
     return (resist, mask_grad)
 
 

time: 134 us -> 130 us (0.970)
  waiting for transfers between devices: 27.6 us -> 23.8 us
  starting transfers between devices: 13.1 us -> 14.8 us
    all_gather x1 -> x0, waiting for transfers between devices: 14.5 us -> none  [local(): lax.all_gather(settled, 'tile', axis=1, tiled=True)]
    ppermute x0 -> x3, waiting for transfers between devices: none -> 10.1 us  [the longest x2 9.72 us: local(): w_next = jax.lax.ppermute(w_next, axis_name='tile', perm=slots)]
    ppermute x0 -> x3, starting transfers between devices: none -> 1.79 us  [the longest x1 1.73 us: local(): f_now = jax.lax.ppermute(f_now, axis_name='tile', perm=steps_seen)]
    unnamed x10 -> x12, local copies, waits for them, and re-layouts: 3.42 us -> 2.44 us
    while x16 -> x8, local copies, waits for them, and re-layouts: 4.44 us -> 4.43 us
  transfers between devices with their start and end apart: 4 -> 6, of which waited for: 4 -> 6; matrix products, arithmetic and copies ran while one was open for 5% -> 6% of each run, Pallas kernels for 0% -> 0%
where the time goes in v1:
time: 130 us
  blocking collectives  30.9 us (24%)
  waiting for transfers between devices  23.8 us (18%)
  other arithmetic  22.1 us (17%)
  starting transfers between devices  14.8 us (11%)
  between operations  14.4 us (11%)
  matrix products  12.9 us (10%)
  local copies, waits for them, and re-layouts  10.7 us (8%)
    psum x1, blocking collectives, local(): lax.psum(grad_part.astype(jnp.bfloat16), 'tile').astype(jnp.float32)  10.4 us
    psum x1, blocking collectives, local(): spectra = lax.psum(partial_value.astype(jnp.bfloat16), 'tile')  10.4 us
    all_to_all x1, blocking collectives, local(): lax.all_to_all(returned.astype(jnp.bfloat16), 'ctx', split_axis=0, concat...  10.1 us
    ppermute x2, waiting for transfers between devices, local(): w_next = jax.lax.ppermute(w_next, axis_name='tile', perm=slots)  9.72 us
    sub x4, other arithmetic, complex_times(): factor_real * values_real - factor_imag * values_imag  8.64 us
    another operation x6, other arithmetic  7.55 us
    all_to_all x1, starting transfers between devices, local(): lax.all_to_all(wanted[:, None], 'ctx', split_axis=0, concat_axis=0, tiled...  7.31 us
    all_to_all x1, waiting for transfers between devices, local(): lax.all_to_all(outgoing, 'ctx', split_axis=0, concat_axis=0, tiled=True)  7.22 us
  transfers between devices with their start and end apart: 6, of which 6 were waited for; matrix products, arithmetic and copies ran while one was open for 6% of the time, Pallas kernels for 0%

profile of v1, /device:TPU:0, one launch (start us, length us, event | category | flops | bytes accessed | tf_op | source)
XLA Modules:
  0.0 129.9 jit_solution(5920911471340869207)
XLA Ops:
  7.2 2.2 %convolution_convert_fusion.4 = bf16[2,128,512]{2,1,0:T(8,128)(2,1)} fusion(bf16[2,128,512]{2,1,0:T(8,128)(2,1)} %param.9, bf16[512,512]{1,0:T(8,128)(2,1)} %param.11), kind=kOutput, calls=%fused_computation.60 | convolution fusion | flops 134348800 | bytes 1048576 | tf_op jit(solution)/shard_map/mxy,zy->mxz/dot_general | solution.py:133
  9.5 0.7 and_select_fusion.1
  10.4 0.7 copy.89
  11.1 7.3 %all-to-all-start = ((s32[8,1,1]{2,1,0:T(1,128)}), s32[8,1,1]{2,1,0:T(1,128)S(1)}, u32[]{:S(2)}, u32[]{:S(2)}) async-start(s32[8,1,1]{2,1,0:T(1,128)} %copy.89), calls=%async_computation | async-start | bytes 8192 | tf_op jit(solution)/shard_map/all_to_all | solution.py:129
  18.5 0.7 copy.87
  19.3 1.1 fusion.46
  21.4 1.1 cosine_multiply_fusion
  22.9 2.0 %all-to-all-done = s32[8,1,1]{2,1,0:T(1,128)S(1)} async-done(((s32[8,1,1]{2,1,0:T(1,128)}), s32[8,1,1]{2,1,0:T(1,128)S(1)}, u32[]{:S(2)}, u32[]{:S(2)}) %all-to-all-start) | async-done | bytes 64 | tf_op jit(solution)/shard_map/all_to_all | solution.py:129
  25.1 4.5 %all-gather.2.cloned.1.call-done = bf16[2,512,512]{2,1,0:T(8,128)(2,1)} async-done(((bf16[2,128,512]{2,1,0:T(8,128)(2,1)}), bf16[2,512,512]{2,1,0:T(8,128)(2,1)}) %all-gather.2.cloned.1.call-update) | async-done | bytes 1048592 | tf_op jit(solution)/shard_map/all_gather | solution.py:140
  29.6 1.9 %fusion.27 = bf16[2,128,128]{2,1,0:T(8,128)(2,1)S(1)} fusion(bf16[2,512,512]{2,1,0:T(8,128)(2,1)} %all-gather.2.cloned.1.call-done, bf16[512,128]{1,0:T(8,128)(2,1)S(1)} %maximum_convert_fusion, bf16[512,512]{1,0:T(8,128)(2,1)S(1)} %copy-done, s32[]{:T(128)S(6)} %select_n.172), kind=kOutput, calls=%fused_computation.68 | convolution fusion | flops 167936000 | bytes 1376260 | tf_op jit(solution)/shard_map/mxy,yv->mxv/dot_general | solution.py:143
  32.0 10.4 %psum.14 = bf16[2,64,128]{2,1,0:T(8,128)(2,1)S(1)} all-reduce(bf16[2,64,128]{2,1,0:T(8,128)(2,1)S(1)} %pad_maximum_fusion.1), channel_id=1, replica_groups=mesh['ctx'=8,'tile'=4] {'tile'}, use_global_device_ids=true, to_apply=%region_1.2 | all-reduce | flops 16384 | bytes 65536 | tf_op jit(solution)/shard_map/psum | solution.py:147
  42.7 0.7 copy.93
  43.4 5.7 %all-to-all-start.1 = ((bf16[8,64,128]{2,1,0:T(8,128)(2,1)}), bf16[8,64,128]{2,1,0:T(8,128)(2,1)S(1)}, u32[]{:S(2)}, u32[]{:S(2)}) async-start(bf16[8,64,128]{2,1,0:T(8,128)(2,1)} %copy.93), calls=%async_computation.1 | async-start | bytes 262144 | tf_op jit(solution)/shard_map/all_to_all | solution.py:151
  49.2 7.2 %all-to-all-done.1 = bf16[8,64,128]{2,1,0:T(8,128)(2,1)S(1)} async-done(((bf16[8,64,128]{2,1,0:T(8,128)(2,1)}), bf16[8,64,128]{2,1,0:T(8,128)(2,1)S(1)}, u32[]{:S(2)}, u32[]{:S(2)}) %all-to-all-start.1) | async-done | bytes 131104 | tf_op jit(solution)/shard_map/all_to_all | solution.py:151
  57.3 4.6 %multiply_subtract_fusion.2 = (f32[24,64,64]{2,0,1:T(8,128)S(1)}, f32[24,64,64]{2,0,1:T(8,128)S(1)}) fusion(f32[24,64,128]{2,0,1:T(8,128)S(1)} %fusion.36, s32[24,64]{1,0:T(8,128)S(1)} %get-tuple-element.289, s32[24,64]{0,1:T(8,128)S(1)} %copy.88), kind=kLoop, calls=%fused_computation.82 | loop fusion | flops 2064384 | bytes 1585152 | tf_op jit(solution)/shard_map/sub | solution.py:64
  62.4 0.7 copy-done.5
  63.1 19.3 %while.14 = (s32[]{:T(128)}, bf16[2,128,512]{2,1,0:T(8,128)(2,1)S(1)}, bf16[2,64,128]{2,1,0:T(8,128)(2,1)S(1)}, f32[6,64,128]{2,1,0:T(8,128)S(1)}, f32[2,64,128]...) while((s32[]{:T(128)}, ...), condition=%wide.region_6.7_spmd, body=%wide.region_3.6_spmd.sunk | while | flops 538632192 | bytes 55263464 | solution.py:175
  64.4 0.6 convolution_bitcast_fusion.11
  65.0 1.0 copy-done.1
  66.5 1.2 copy-done.2
  68.2 3.3 %multiply_convert_fusion.4 = (bf16[6,128,512]{1,2,0:T(8,128)(2,1)S(1)}, bf16[6,128,512]{1,2,0:T(8,128)(2,1)S(1)}) fusion(f32[128,512]{0,1:T(8,128)S(1)} %fusion.140, f32[6,128,1024]{1,2,0:T(8,128)} %copy-done.1, f32[6,128,1024]{1,2,0:T(8,128)} %copy-done.2), kind=kLoop, calls=%fused_computation.10.clone.1 | loop fusion | flops 2359296 | bytes 8126464 | tf_op jit(solution)/shard_map/convert
  74.1 0.6 convolution_bitcast_fusion.11
  74.7 1.0 copy-done.1
  76.1 1.2 copy-done.2
  77.8 3.3 %multiply_convert_fusion.4 = (bf16[6,128,512]{1,2,0:T(8,128)(2,1)S(1)}, bf16[6,128,512]{1,2,0:T(8,128)(2,1)S(1)}) fusion(f32[128,512]{0,1:T(8,128)S(1)} %fusion.140, f32[6,128,1024]{1,2,0:T(8,128)} %copy-done.1, f32[6,128,1024]{1,2,0:T(8,128)} %copy-done.2), kind=kLoop, calls=%fused_computation.10.clone.1 | loop fusion | flops 2359296 | bytes 8126464 | tf_op jit(solution)/shard_map/convert
  82.4 10.4 %psum.15 = bf16[2,64,128]{2,1,0:T(8,128)(2,1)S(1)} all-reduce(bf16[2,64,128]{2,1,0:T(8,128)(2,1)S(1)} %get-tuple-element.159), channel_id=1, replica_groups=mesh['ctx'=8,'tile'=4] {'tile'}, use_global_device_ids=true, to_apply=%region_7.8 | all-reduce | flops 16384 | bytes 65536 | tf_op jit(solution)/shard_map/psum | solution.py:176
  93.3 3.6 %multiply_subtract_fusion.1 = (f32[24,64,64]{2,0,1:T(8,128)S(1)}, f32[24,64,64]{2,0,1:T(8,128)S(1)}) fusion(f32[24,64,64]{2,1,0:T(8,128)S(1)} %get-tuple-element.276, f32[24,64,64]{2,1,0:T(8,128)S(1)} %get-tuple-element.275, s32[24,64]{1,0:T(8,128)S(1)} %get-tuple-element.289, s32[24,64]{0,1:T(8,128)S(1)} %copy.88), kind=kLoop, calls=%fused_computation.80 | loop fusion | flops 1966080 | bytes 1585152 | tf_op jit(solution)/shard_map/sub | solution.py:64
  97.5 10.1 %all_to_all.19 = bf16[8,64,128]{2,1,0:T(8,128)(2,1)S(1)} all-to-all(bf16[8,64,128]{2,1,0:T(8,128)(2,1)S(1)} %copy.101), channel_id=1, replica_groups=mesh['ctx'=8,'tile'=4] {'ctx'}, dimensions={0} | all-to-all | bytes 262144 | tf_op jit(solution)/shard_map/all_to_all | solution.py:185
  109.0 1.7 %collective-permute-start = (bf16[2,128,512]{2,1,0:T(8,128)(2,1)S(1)}, bf16[2,128,512]{2,1,0:T(8,128)(2,1)S(1)}, u32[]{:S(2)}, u32[]{:S(2)}) collective-permute-start(bf16[2,128,512]{2,1,0:T(8,128)(2,1)S(1)} %convolution_convert_fusion.1), channel_id=1, source_target_pairs={{0,3},{1,0},{2,1},{3,2},{4,7},{5,4},{6,5},{7,6},{8,11},{9,8},{10,9... | collective-permute-start | bytes 786440 | tf_op jit(solution)/shard_map/ppermute | solution.py:222
  111.0 5.0 %collective-permute-done.1 = bf16[2,128,512]{2,1,0:T(8,128)(2,1)S(1)} collective-permute-done((bf16[2,128,512]{2,1,0:T(8,128)(2,1)S(1)}, bf16[2,128,512]{2,1,0:T(8,128)(2,1)S(1)}, u32[]{:S(2)}, u32[]{:S(2)}) %collective-permute-start.1) | collective-permute-done | bytes 262176 | tf_op jit(solution)/shard_map/ppermute | solution.py:220
  117.0 4.8 %collective-permute-done.2 = bf16[2,128,512]{2,1,0:T(8,128)(2,1)S(1)} collective-permute-done((bf16[2,128,512]{2,1,0:T(8,128)(2,1)S(1)}, bf16[2,128,512]{2,1,0:T(8,128)(2,1)S(1)}, u32[]{:S(2)}, u32[]{:S(2)}) %collective-permute-start.2) | collective-permute-done | bytes 262176 | tf_op jit(solution)/shard_map/ppermute | solution.py:220
  122.1 1.0 copy.112
  (98 shorter events, 15.0 us)
Async XLA Ops:
  7.2 22.4 %copy-start = (bf16[512,512]{1,0:T(8,128)(2,1)S(1)}, bf16[512,512]{1,0:T(8,128)(2,1)}, u32[]{:S(2)}) copy-start(bf16[512,512]{1,0:T(8,128)(2,1)} %param.10) | copy-start | bytes 1572868
  7.2 22.4 %all-gather.2.cloned.1.call-start = ((), (), s32[]{:S(2)}) async-start(), calls=%async_computation.3 | async-start | bytes 1310720 | tf_op jit(solution)/shard_map/all_gather | solution.py:140
  11.1 13.7 %all-to-all-start = ((s32[8,1,1]{2,1,0:T(1,128)}), s32[8,1,1]{2,1,0:T(1,128)S(1)}, u32[]{:S(2)}, u32[]{:S(2)}) async-start(s32[8,1,1]{2,1,0:T(1,128)} %copy.89), calls=%async_computation | async-start | bytes 8192 | tf_op jit(solution)/shard_map/all_to_all | solution.py:129
  22.8 26.3 %copy-start.3 = (f32[6,64,128]{2,1,0:T(8,128)S(1)}, f32[6,64,128]{2,1,0:T(8,128)}, u32[]{:S(2)}) copy-start(f32[6,64,128]{2,1,0:T(8,128)} %param.12) | copy-start | bytes 589828
  43.4 13.0 %all-to-all-start.1 = ((bf16[8,64,128]{2,1,0:T(8,128)(2,1)}), bf16[8,64,128]{2,1,0:T(8,128)(2,1)S(1)}, u32[]{:S(2)}, u32[]{:S(2)}) async-start(bf16[8,64,128]{2,1,0:T(8,128)(2,1)} %copy.93), calls=%async_computation.1 | async-start | bytes 262144 | tf_op jit(solution)/shard_map/all_to_all | solution.py:151
  62.2 1.0 copy-start.5
  64.4 1.6 %copy-start.1 = (f32[6,128,1024]{1,2,0:T(8,128)}, f32[6,128,1024]{1,2,0:T(8,128)S(1)}, u32[]{:S(2)}) copy-start(f32[6,128,1024]{1,2,0:T(8,128)S(1)} %convolution_bitcast_fusion.10) | copy-start | bytes 9437188 | tf_op jit(solution)/shard_map/while
  66.0 1.7 %copy-start.2 = (f32[6,128,1024]{1,2,0:T(8,128)}, f32[6,128,1024]{1,2,0:T(8,128)S(1)}, u32[]{:S(2)}) copy-start(f32[6,128,1024]{1,2,0:T(8,128)S(1)} %convolution_bitcast_fusion.11) | copy-start | bytes 9437188 | tf_op jit(solution)/shard_map/while
  74.0 1.6 %copy-start.1 = (f32[6,128,1024]{1,2,0:T(8,128)}, f32[6,128,1024]{1,2,0:T(8,128)S(1)}, u32[]{:S(2)}) copy-start(f32[6,128,1024]{1,2,0:T(8,128)S(1)} %convolution_bitcast_fusion.10) | copy-start | bytes 9437188 | tf_op jit(solution)/shard_map/while
  75.7 1.7 %copy-start.2 = (f32[6,128,1024]{1,2,0:T(8,128)}, f32[6,128,1024]{1,2,0:T(8,128)S(1)}, u32[]{:S(2)}) copy-start(f32[6,128,1024]{1,2,0:T(8,128)S(1)} %convolution_bitcast_fusion.11) | copy-start | bytes 9437188 | tf_op jit(solution)/shard_map/while
  82.4 10.9 %copy-start.6 = (bf16[2,128,512]{2,1,0:T(8,128)(2,1)}, bf16[2,128,512]{2,1,0:T(8,128)(2,1)S(1)}, u32[]{:S(2)}) copy-start(bf16[2,128,512]{2,1,0:T(8,128)(2,1)S(1)} %get-tuple-element.233) | copy-start | bytes 786436
  97.5 10.8 %copy-start.4 = (bf16[512,512]{1,0:T(8,128)(2,1)S(1)}, bf16[512,512]{1,0:T(8,128)(2,1)}, u32[]{:S(2)}) copy-start(bf16[512,512]{1,0:T(8,128)(2,1)} %param.11) | copy-start | bytes 1572868
  108.9 7.1 %collective-permute-start.1 = (bf16[2,128,512]{2,1,0:T(8,128)(2,1)S(1)}, bf16[2,128,512]{2,1,0:T(8,128)(2,1)S(1)}, u32[]{:S(2)}, u32[]{:S(2)}) collective-permute-start(bf16[2,128,512]{2,1,0:T(8,128)(2,1)S(1)} %convolution_convert_fusion.1), channel_id=1, source_target_pairs={{0,1},{1,2},{2,3},{3,0},{4,5},{5,6},{6,7},{7,4},{8,9},{9,10},{10,1... | collective-permute-start | bytes 786440 | tf_op jit(solution)/shard_map/ppermute | solution.py:220
  109.0 7.4 %collective-permute-start = (bf16[2,128,512]{2,1,0:T(8,128)(2,1)S(1)}, bf16[2,128,512]{2,1,0:T(8,128)(2,1)S(1)}, u32[]{:S(2)}, u32[]{:S(2)}) collective-permute-start(bf16[2,128,512]{2,1,0:T(8,128)(2,1)S(1)} %convolution_convert_fusion.1), channel_id=1, source_target_pairs={{0,3},{1,0},{2,1},{3,2},{4,7},{5,4},{6,5},{7,6},{8,11},{9,8},{10,9... | collective-permute-start | bytes 786440 | tf_op jit(solution)/shard_map/ppermute | solution.py:222
  116.0 5.8 %collective-permute-start.2 = (bf16[2,128,512]{2,1,0:T(8,128)(2,1)S(1)}, bf16[2,128,512]{2,1,0:T(8,128)(2,1)S(1)}, u32[]{:S(2)}, u32[]{:S(2)}) collective-permute-start(bf16[2,128,512]{2,1,0:T(8,128)(2,1)S(1)} %collective-permute-done.1), channel_id=1, source_target_pairs={{0,1},{1,2},{2,3},{3,0},{4,5},{5,6},{6,7},{7,4},{8,9},{9,10},{10,1... | collective-permute-start | bytes 786440 | tf_op jit(solution)/shard_map/ppermute | solution.py:220
Sparse Core Ops, SparseCore 0:
  10.1 19.4 all-gather.1
